TPU v7x, 32 devices: a whole 2x2x4 slice. The times are simulated.
32 devices in a mesh: prow: 4 (over y, core), pcol: 8 (over z, x).
Axes of the slice: x: 2, y: 2, z: 4, core: 2. Of those that a mesh axis runs over, the one named last changes fastest.
Arguments:
- vectors: bfloat16 [512, 120064], P('pcol', 'prow'), may hold values from -6 to 6
- reflectors: bfloat16 [2, 256, 120064], P(None, 'pcol', 'prow'), may hold values from -6 to 6
- panel_factor: float32 [2, 256, 256], replicated, as said below
Outputs:
- band_vectors: bfloat16 [8, 64, 120064], P('pcol', 'prow')
Inputs may be any that keep to these rules, and one draw needn't show every extreme that they name: `panel_factor`: upper triangular: zero below the diagonal; diagonal entries between 1 / 120064 and 3 / 120064.
All inputs are finite; a program needn't handle non-finite values.
Results may differ from a plain program's by a relative error of at most 0.0095.
Values may be sent and summed in bfloat16 or wider, within the bound.
No kernel may reach another device: no remote copies, remote signals or barrier semaphores. Data moves between devices by JAX's collectives and lax.ppermute only.
A program may use at most 192 MiB of HBM per device.

v0:
```python
import jax
import jax.numpy as jnp
from jax import lax
from jax.sharding import PartitionSpec as P


def finish_panel(current, panel, factor, projected):
    scaled = lax.dot_general(
        projected,
        factor,
        (((1,), (1,)), ((), ())),
        precision=lax.Precision.HIGHEST,
        preferred_element_type=jnp.float32,
    ).astype(jnp.bfloat16)
    updated = current.astype(jnp.float32) - jnp.dot(
        scaled, panel, preferred_element_type=jnp.float32
    )
    return updated.astype(jnp.bfloat16)


def partial_products(current, panel):
    return lax.dot_general(
        current, panel, (((1,), (1,)), ((), ())), preferred_element_type=jnp.float32
    )


def apply_panel(current, panel, factor):
    partial_sum = partial_products(current, panel)
    projected = lax.psum(partial_sum.astype(jnp.bfloat16), "prow").astype(jnp.float32)
    return finish_panel(current, panel, factor, projected)


def body(vectors, reflectors, panel_factor):
    current = vectors
    for number in range(reflectors.shape[0]):
        single = lax.all_gather(reflectors[number], "pcol", axis=0, tiled=True)
        current = apply_panel(current, single, panel_factor[number])
    owned_rows = lax.all_to_all(current, "prow", split_axis=0, concat_axis=1, tiled=True)
    return owned_rows[None]


def solution(mesh):
    placed = (P("pcol", "prow"), P(None, "pcol", "prow"), P())
    return jax.shard_map(
        body, mesh=mesh, in_specs=placed, out_specs=P("pcol", "prow", None), check_vma=False
    )
```

profile of v0, /device:TPU:0, one launch (start us, length us, event | category | flops | bytes accessed | tf_op | source)
XLA Modules:
  0.0 529.0 jit_solution(264437417981960315)
XLA Ops:
  6.5 0.0 all-gather.5.cloned.1.call-start
  6.5 4.2 fusion.18
  10.8 0.0 all-gather.5.cloned.1.call-update
  10.8 0.0 all-gather.7.cloned.1.call-start
  10.9 0.7 all-gather.7.cloned.1.call-update
  11.6 0.0 copy-start
  11.6 212.6 %all-gather.5.cloned.1.call-done = bf16[1,256,30016]{2,1,0:T(8,128)(2,1)} async-done(((bf16[1,32,30016]{2,1,0:T(8,128)(2,1)}), bf16[1,256,30016]{2,1,0:T(8,128)(2,1)}) %all-gather.5.cloned.1.call-update) | async-done | bytes 15368208 | tf_op jit(solution)/shard_map/all_gather | solution.py:36
  224.2 11.2 %fusion.8 = bf16[64,256]{1,0:T(8,128)(2,1)S(1)} fusion(bf16[64,30016]{1,0:T(8,128)(2,1)} %param.3, bf16[1,256,30016]{2,1,0:T(8,128)(2,1)} %all-gather.5.cloned.1.call-done), kind=kOutput, calls=%fused_computation.10 | convolution fusion | flops 983580672 | bytes 19243008 | tf_op jit(solution)/shard_map/dot_general | solution.py:22
  235.4 11.2 %psum.14 = bf16[64,256]{1,0:T(8,128)(2,1)S(1)} all-reduce(bf16[64,256]{1,0:T(8,128)(2,1)S(1)} %fusion.8), channel_id=1, replica_groups=mesh['prow'=4,'pcol'=8] {'prow'}, use_global_device_ids=true, to_apply=%region_0.0 | all-reduce | flops 16384 | bytes 65536 | tf_op jit(solution)/shard_map/psum | solution.py:29
  246.6 0.0 copy-done
  246.6 0.3 convolution_convert_fusion.1
  246.9 10.6 %fusion = bf16[64,30016]{1,0:T(8,128)(2,1)} fusion(bf16[64,256]{1,0:T(8,128)(2,1)S(1)} %convolution_convert_fusion.1, bf16[1,256,30016]{2,1,0:T(8,128)(2,1)} %all-gather.5.cloned.1.call-done, bf16[64,30016]{1,0:T(8,128)(2,1)} %param.3), kind=kOutput, calls=%fused_computation.2 | convolution fusion | flops 989327360 | bytes 23085056 | tf_op jit(solution)/shard_map/dot_general | solution.py:15
  257.5 177.6 %all-gather.7.cloned.1.call-done = bf16[1,256,30016]{2,1,0:T(8,128)(2,1)} async-done(((bf16[1,32,30016]{2,1,0:T(8,128)(2,1)}), bf16[1,256,30016]{2,1,0:T(8,128)(2,1)}) %all-gather.7.cloned.1.call-update) | async-done | bytes 15368208 | tf_op jit(solution)/shard_map/all_gather | solution.py:36
  435.0 11.2 %fusion.11 = bf16[64,256]{1,0:T(8,128)(2,1)S(1)} fusion(bf16[64,30016]{1,0:T(8,128)(2,1)} %fusion, bf16[1,256,30016]{2,1,0:T(8,128)(2,1)} %all-gather.7.cloned.1.call-done), kind=kOutput, calls=%fused_computation.11 | convolution fusion | flops 983580672 | bytes 19243008 | tf_op jit(solution)/shard_map/dot_general | solution.py:22
  446.3 10.4 %psum.15 = bf16[64,256]{1,0:T(8,128)(2,1)S(1)} all-reduce(bf16[64,256]{1,0:T(8,128)(2,1)S(1)} %fusion.11), channel_id=1, replica_groups=mesh['prow'=4,'pcol'=8] {'prow'}, use_global_device_ids=true, to_apply=%region_1.0 | all-reduce | flops 16384 | bytes 65536 | tf_op jit(solution)/shard_map/psum | solution.py:29
  456.6 0.3 convolution_convert_fusion
  456.9 8.7 %fusion.1 = bf16[64,30016]{1,0:T(8,128)(2,1)S(1)} fusion(bf16[64,256]{1,0:T(8,128)(2,1)S(1)} %convolution_convert_fusion, bf16[1,256,30016]{2,1,0:T(8,128)(2,1)} %all-gather.7.cloned.1.call-done, bf16[64,30016]{1,0:T(8,128)(2,1)} %fusion), kind=kOutput, calls=%fused_computation.3 | convolution fusion | flops 989327360 | bytes 23085056 | tf_op jit(solution)/shard_map/dot_general | solution.py:15
  465.6 47.1 %all_to_all.16 = bf16[4,16,30016]{2,1,0:T(8,128)(2,1)S(1)} all-to-all(bf16[4,16,30016]{2,1,0:T(8,128)(2,1)S(1)} %bitcast.28), channel_id=1, replica_groups=mesh['prow'=4,'pcol'=8] {'prow'}, dimensions={0} | all-to-all | bytes 7684096 | tf_op jit(solution)/shard_map/all_to_all | solution.py:38
  512.7 3.3 copy.4
  516.0 6.2 %broadcast_in_dim.3 = bf16[1,16,120064]{2,1,0:T(8,128)(2,1)} reshape(bf16[16,4,30016]{2,1,0:T(4,128)(2,1)} %copy.4) | data formatting | bytes 7684096 | tf_op jit(solution)/shard_map/broadcast_in_dim | solution.py:39
Async XLA Ops:
  6.5 217.6 %all-gather.5.cloned.1.call-start = ((), (), s32[]{:S(2)}) async-start(), calls=%async_computation.1 | async-start | bytes 17326080 | tf_op jit(solution)/shard_map/all_gather | solution.py:36
  10.8 424.2 %all-gather.7.cloned.1.call-start = ((), (), s32[]{:S(2)}) async-start(), calls=%async_computation.2 | async-start | bytes 17326080 | tf_op jit(solution)/shard_map/all_gather | solution.py:36
  11.6 235.0 %copy-start = (f32[2,256,256]{2,1,0:T(8,128)S(1)}, f32[2,256,256]{2,1,0:T(8,128)}, u32[]{:S(2)}) copy-start(f32[2,256,256]{2,1,0:T(8,128)} %param.5) | copy-start | bytes 1572868
Sparse Core Ops, SparseCore 0:
  10.9 213.1 all-gather.4
  226.3 208.6 all-gather.6
where the time goes:
time: 529 us
  waiting for transfers between devices  391 us (74%)
  blocking collectives  68.6 us (13%)
  matrix products  42.3 us (8%)
  local copies, waits for them, and re-layouts  13.8 us (3%)
  between operations  13.5 us (3%)
    all_gather x2, waiting for transfers between devices, body(): single = lax.all_gather(reflectors[number], 'pcol', axis=0, tiled=True)  390 us
    all_to_all x1, blocking collectives, body(): lax.all_to_all(current, 'prow', split_axis=0, concat_axis=1, tiled=True)  47.1 us
    dot_general x2, matrix products, partial_products(): lax.dot_general(current, panel, (((1,), (1,)), ((), ())), preferred_eleme...  22.5 us
    psum x2, blocking collectives, apply_panel(): lax.psum(partial_sum.astype(jnp.bfloat16), 'prow').astype(jnp.float32)  21.5 us
    dot_general x2, matrix products, finish_panel(): jnp.dot(scaled, panel, preferred_element_type=jnp.float32)  19.3 us
  transfers between devices with their start and end apart: 2, of which 2 were waited for; matrix products, arithmetic and copies ran while one was open for 4% of the time, Pallas kernels for 0%

commit v1 on v0

--- a/solution.py
+++ b/solution.py
@@ -2,6 +2,20 @@
 import jax.numpy as jnp
 from jax import lax
 from jax.sharding import PartitionSpec as P
+
+
+def mark_the_halves(packet, net_axis):
+    dev_n = lax.psum(1, net_axis)
+    trail = [packet]
+    j0 = 0
+    while j0 < dev_n - 1:
+        trail.append(
+            lax.ppermute(trail[-1], net_axis, [(dd, (dd + 1) % dev_n) for dd in range(dev_n)])
+        )
+        j0 += 1
+    clean = jnp.concatenate(trail[::-1], 0)
+    n_now = lax.axis_index(net_axis)
+    return jnp.roll(clean, (n_now + 1) * packet.shape[0], 0)
 
 
 def finish_panel(current, panel, factor, projected):
@@ -33,7 +47,7 @@
 def body(vectors, reflectors, panel_factor):
     current = vectors
     for number in range(reflectors.shape[0]):
-        single = lax.all_gather(reflectors[number], "pcol", axis=0, tiled=True)
+        single = mark_the_halves(reflectors[number], "pcol")
         current = apply_panel(current, single, panel_factor[number])
     owned_rows = lax.all_to_all(current, "prow", split_axis=0, concat_axis=1, tiled=True)
     return owned_rows[None]

time: 529 us -> 736 us (1.39)
  waiting for transfers between devices: 391 us -> 568 us
  local copies, waits for them, and re-layouts: 13.8 us -> 43.6 us
  between operations: 13.5 us -> 0.2 us
  matrix products: 42.3 us -> 51 us
    ppermute x0 -> x14, waiting for transfers between devices: none -> 568 us  [mark_the_halves(): lax.ppermute(trail[-1], net_axis, [(dd, (dd + 1) % dev_n) for dd in range...]
    all_gather x2 -> x0, waiting for transfers between devices: 390 us -> none  [body(): single = lax.all_gather(reflectors[number], 'pcol', axis=0, tiled=True)]
    unnamed x2 -> x48, local copies, waits for them, and re-layouts: 0.01 us -> 30.2 us
    dot_general x2, matrix products: 19.3 us -> 29 us  [finish_panel(): jnp.dot(scaled, panel, preferred_element_type=jnp.float32)]
  transfers between devices with their start and end apart: 2 -> 14, of which waited for: 2 -> 14; matrix products, arithmetic and copies ran while one was open for 4% -> 1% of each run, Pallas kernels for 0% -> 0%
where the time goes in v1:
time: 736 us
  waiting for transfers between devices  568 us (77%)
  blocking collectives  68.6 us (9%)
  matrix products  51 us (7%)
  local copies, waits for them, and re-layouts  43.6 us (6%)
    ppermute x14, waiting for transfers between devices, mark_the_halves(): lax.ppermute(trail[-1], net_axis, [(dd, (dd + 1) % dev_n) for dd in range...  568 us
    all_to_all x1, blocking collectives, body(): lax.all_to_all(current, 'prow', split_axis=0, concat_axis=1, tiled=True)  47 us
    unnamed x48, local copies, waits for them, and re-layouts  30.2 us
    dot_general x2, matrix products, finish_panel(): jnp.dot(scaled, panel, preferred_element_type=jnp.float32)  29 us
    psum x2, blocking collectives, apply_panel(): lax.psum(partial_sum.astype(jnp.bfloat16), 'prow').astype(jnp.float32)  21.7 us
    dot_general x2, matrix products, partial_products(): lax.dot_general(current, panel, (((1,), (1,)), ((), ())), preferred_eleme...  21.4 us
  transfers between devices with their start and end apart: 14, of which 14 were waited for; matrix products, arithmetic and copies ran while one was open for 1% of the time, Pallas kernels for 0%

profile of v1, /device:TPU:0, one launch (start us, length us, event | category | flops | bytes accessed | tf_op | source)
XLA Modules:
  0.0 735.7 jit_solution(15256260329332660349)
XLA Ops:
  0.0 2.4 slice_bitcast_fusion
  2.4 3.0 collective-permute-start
  5.4 1.5 collective-permute-start.7
  6.9 44.3 %collective-permute-done = bf16[32,30016]{1,0:T(8,128)(2,1)S(1)} collective-permute-done((bf16[32,30016]{1,0:T(8,128)(2,1)S(1)}, bf16[32,30016]{1,0:T(8,128)(2,1)S(1)}, u32[]{:S(2)}, u32[]{:S(2)}) %collective-permute-start) | collective-permute-done | bytes 1921056 | tf_op jit(solution)/shard_map/ppermute | solution.py:13
  51.2 0.0 collective-permute-start.1
  51.2 41.2 %collective-permute-done.7 = bf16[32,30016]{1,0:T(8,128)(2,1)S(1)} collective-permute-done((bf16[32,30016]{1,0:T(8,128)(2,1)S(1)}, bf16[32,30016]{1,0:T(8,128)(2,1)S(1)}, u32[]{:S(2)}, u32[]{:S(2)}) %collective-permute-start.7) | collective-permute-done | bytes 1921056 | tf_op jit(solution)/shard_map/ppermute | solution.py:13
  92.5 0.0 collective-permute-start.8
  92.5 41.3 %collective-permute-done.1 = bf16[32,30016]{1,0:T(8,128)(2,1)S(1)} collective-permute-done((bf16[32,30016]{1,0:T(8,128)(2,1)S(1)}, bf16[32,30016]{1,0:T(8,128)(2,1)S(1)}, u32[]{:S(2)}, u32[]{:S(2)}) %collective-permute-start.1) | collective-permute-done | bytes 1921056 | tf_op jit(solution)/shard_map/ppermute | solution.py:13
  133.7 0.0 collective-permute-start.2
  133.7 41.2 %collective-permute-done.8 = bf16[32,30016]{1,0:T(8,128)(2,1)S(1)} collective-permute-done((bf16[32,30016]{1,0:T(8,128)(2,1)S(1)}, bf16[32,30016]{1,0:T(8,128)(2,1)S(1)}, u32[]{:S(2)}, u32[]{:S(2)}) %collective-permute-start.8) | collective-permute-done | bytes 1921056 | tf_op jit(solution)/shard_map/ppermute | solution.py:13
  175.0 0.0 copy-done.1
  175.0 0.0 collective-permute-start.9
  175.0 1.2 copy-done.3
  176.2 40.0 %collective-permute-done.2 = bf16[32,30016]{1,0:T(8,128)(2,1)S(1)} collective-permute-done((bf16[32,30016]{1,0:T(8,128)(2,1)S(1)}, bf16[32,30016]{1,0:T(8,128)(2,1)S(1)}, u32[]{:S(2)}, u32[]{:S(2)}) %collective-permute-start.2) | collective-permute-done | bytes 1921056 | tf_op jit(solution)/shard_map/ppermute | solution.py:13
  216.2 0.0 collective-permute-start.3
  216.2 41.2 %collective-permute-done.9 = bf16[32,30016]{1,0:T(8,128)(2,1)S(1)} collective-permute-done((bf16[32,30016]{1,0:T(8,128)(2,1)S(1)}, bf16[32,30016]{1,0:T(8,128)(2,1)S(1)}, u32[]{:S(2)}, u32[]{:S(2)}) %collective-permute-start.9) | collective-permute-done | bytes 1921056 | tf_op jit(solution)/shard_map/ppermute | solution.py:13
  257.5 0.0 copy-done.5
  257.5 0.0 collective-permute-start.10
  257.5 1.3 copy-done.7
  258.8 40.0 %collective-permute-done.3 = bf16[32,30016]{1,0:T(8,128)(2,1)S(1)} collective-permute-done((bf16[32,30016]{1,0:T(8,128)(2,1)S(1)}, bf16[32,30016]{1,0:T(8,128)(2,1)S(1)}, u32[]{:S(2)}, u32[]{:S(2)}) %collective-permute-start.3) | collective-permute-done | bytes 1921056 | tf_op jit(solution)/shard_map/ppermute | solution.py:13
  298.7 0.0 collective-permute-start.4
  298.7 41.2 %collective-permute-done.10 = bf16[32,30016]{1,0:T(8,128)(2,1)S(1)} collective-permute-done((bf16[32,30016]{1,0:T(8,128)(2,1)S(1)}, bf16[32,30016]{1,0:T(8,128)(2,1)S(1)}, u32[]{:S(2)}, u32[]{:S(2)}) %collective-permute-start.10) | collective-permute-done | bytes 1921056 | tf_op jit(solution)/shard_map/ppermute | solution.py:13
  340.0 0.0 copy-done.9
  340.0 0.0 collective-permute-start.11
  340.0 1.3 copy-done.11
  341.3 40.0 %collective-permute-done.4 = bf16[32,30016]{1,0:T(8,128)(2,1)S(1)} collective-permute-done((bf16[32,30016]{1,0:T(8,128)(2,1)S(1)}, bf16[32,30016]{1,0:T(8,128)(2,1)S(1)}, u32[]{:S(2)}, u32[]{:S(2)}) %collective-permute-start.4) | collective-permute-done | bytes 1921056 | tf_op jit(solution)/shard_map/ppermute | solution.py:13
  381.3 0.0 collective-permute-start.5
  381.3 41.4 %collective-permute-done.11 = bf16[32,30016]{1,0:T(8,128)(2,1)} collective-permute-done((bf16[32,30016]{1,0:T(8,128)(2,1)S(1)}, bf16[32,30016]{1,0:T(8,128)(2,1)}, u32[]{:S(2)}, u32[]{:S(2)}) %collective-permute-start.11) | collective-permute-done | bytes 1921056 | tf_op jit(solution)/shard_map/ppermute | solution.py:13
  422.6 0.0 collective-permute-start.12
  422.6 41.2 %collective-permute-done.5 = bf16[32,30016]{1,0:T(8,128)(2,1)} collective-permute-done((bf16[32,30016]{1,0:T(8,128)(2,1)S(1)}, bf16[32,30016]{1,0:T(8,128)(2,1)}, u32[]{:S(2)}, u32[]{:S(2)}) %collective-permute-start.5) | collective-permute-done | bytes 1921056 | tf_op jit(solution)/shard_map/ppermute | solution.py:13
  463.9 0.0 collective-permute-start.6
  463.9 41.2 %collective-permute-done.12 = bf16[32,30016]{1,0:T(8,128)(2,1)} collective-permute-done((bf16[32,30016]{1,0:T(8,128)(2,1)}, bf16[32,30016]{1,0:T(8,128)(2,1)}, u32[]{:S(2)}, u32[]{:S(2)}) %collective-permute-start.12) | collective-permute-done | bytes 1921056 | tf_op jit(solution)/shard_map/ppermute | solution.py:13
  505.1 0.0 collective-permute-start.13
  505.1 41.3 %collective-permute-done.6 = bf16[32,30016]{1,0:T(8,128)(2,1)} collective-permute-done((bf16[32,30016]{1,0:T(8,128)(2,1)}, bf16[32,30016]{1,0:T(8,128)(2,1)}, u32[]{:S(2)}, u32[]{:S(2)}) %collective-permute-start.6) | collective-permute-done | bytes 1921056 | tf_op jit(solution)/shard_map/ppermute | solution.py:13
  546.4 1.7 constant_dynamic-update-slice_fusion.7
  548.0 1.8 constant_dynamic-update-slice_fusion.6
  549.8 0.0 copy-start.12
  549.8 1.9 constant_dynamic-update-slice_fusion.5
  551.8 1.9 constant_dynamic-update-slice_fusion.4
  553.7 0.2 constant_dynamic-update-slice_fusion.3
  554.0 0.2 constant_dynamic-update-slice_fusion.2
  554.2 0.0 copy-start
  554.2 0.2 constant_dynamic-update-slice_fusion.1
  554.5 32.2 %collective-permute-done.13 = bf16[32,30016]{1,0:T(8,128)(2,1)S(1)} collective-permute-done((bf16[32,30016]{1,0:T(8,128)(2,1)}, bf16[32,30016]{1,0:T(8,128)(2,1)S(1)}, u32[]{:S(2)}, u32[]{:S(2)}) %collective-permute-start.13) | collective-permute-done | bytes 1921056 | tf_op jit(solution)/shard_map/ppermute | solution.py:13
  586.7 1.4 constant_dynamic-update-slice_fusion.15
  588.1 2.9 constant_dynamic-update-slice_fusion.14
  591.0 2.9 constant_dynamic-update-slice_fusion.13
  593.9 1.4 constant_dynamic-update-slice_fusion.12
  595.3 1.5 constant_dynamic-update-slice_fusion.11
  596.8 1.4 constant_dynamic-update-slice_fusion.10
  598.2 1.5 constant_dynamic-update-slice_fusion.9
  599.7 1.5 constant_dynamic-update-slice_fusion.8
  601.2 5.4 copy-done.16
  606.6 10.0 %fusion.4 = bf16[64,256]{0,1:T(8,128)(2,1)S(1)} fusion(bf16[64,30016]{1,0:T(8,128)(2,1)} %param.5, s32[]{:T(128)S(6)} %select_n.13, bf16[256,30016]{1,0:T(8,128)(2,1)} %copy-done.16), kind=kOutput, calls=%fused_computation.13 | convolution fusion | flops 1014317056 | bytes 19243012 | tf_op jit(solution)/shard_map/dot_general | solution.py:36
  616.6 10.9 %psum.14 = bf16[64,256]{0,1:T(8,128)(2,1)S(1)} all-reduce(bf16[64,256]{0,1:T(8,128)(2,1)S(1)} %fusion.4), channel_id=1, replica_groups=mesh['prow'=4,'pcol'=8] {'prow'}, use_global_device_ids=true, to_apply=%region_0.2 | all-reduce | flops 16384 | bytes 65536 | tf_op jit(solution)/shard_map/psum | solution.py:43
  627.5 0.3 convolution_convert_fusion.3
  627.7 15.1 %fusion = bf16[64,30016]{1,0:T(8,128)(2,1)} fusion(bf16[64,256]{1,0:T(8,128)(2,1)S(1)} %convolution_convert_fusion.3, bf16[64,30016]{1,0:T(8,128)(2,1)} %param.5, s32[]{:T(128)S(6)} %select_n.13, bf16[256,30016]{1,0:T(8,128)(2,1)} %copy-done.16), kind=kOutput, calls=%fused_computation.2 | convolution fusion | flops 1020063744 | bytes 23085060 | tf_op jit(solution)/shard_map/dot_general | solution.py:29
  642.9 11.5 %convolution_convert_fusion.1 = bf16[64,256]{1,0:T(8,128)(2,1)S(1)} fusion(bf16[64,30016]{1,0:T(8,128)(2,1)} %fusion, s32[]{:T(128)S(6)} %select_n.13, bf16[256,30016]{1,0:T(8,128)(2,1)} %get-tuple-element.6), kind=kOutput, calls=%fused_computation.14 | convolution fusion | flops 1014317056 | bytes 19243012 | tf_op jit(solution)/shard_map/dot_general | solution.py:36
  654.3 10.8 %psum.15 = bf16[64,256]{1,0:T(8,128)(2,1)S(1)} all-reduce(bf16[64,256]{1,0:T(8,128)(2,1)S(1)} %convolution_convert_fusion.1), channel_id=1, replica_groups=mesh['prow'=4,'pcol'=8] {'prow'}, use_global_device_ids=true, to_apply=%region_1.3 | all-reduce | flops 16384 | bytes 65536 | tf_op jit(solution)/shard_map/psum | solution.py:43
  665.2 0.3 convolution_convert_fusion.2
  665.4 13.8 %fusion.1 = bf16[64,30016]{1,0:T(8,128)(2,1)S(1)} fusion(bf16[64,256]{1,0:T(8,128)(2,1)S(1)} %convolution_convert_fusion.2, bf16[64,30016]{1,0:T(8,128)(2,1)} %fusion, s32[]{:T(128)S(6)} %select_n.13, bf16[256,30016]{1,0:T(8,128)(2,1)} %get-tuple-element.6), kind=kOutput, calls=%fused_computation.3 | convolution fusion | flops 1020063744 | bytes 23085060 | tf_op jit(solution)/shard_map/dot_general | solution.py:29
  679.3 47.0 %all_to_all.16 = bf16[4,16,30016]{2,1,0:T(8,128)(2,1)S(1)} all-to-all(bf16[4,16,30016]{2,1,0:T(8,128)(2,1)S(1)} %bitcast.25), channel_id=1, replica_groups=mesh['prow'=4,'pcol'=8] {'prow'}, dimensions={0} | all-to-all | bytes 7684096 | tf_op jit(solution)/shard_map/all_to_all | solution.py:52
  726.2 3.3 copy.4
  729.6 6.2 broadcast_in_dim.3
  (25 shorter events, 0.0 us)
Async XLA Ops:
  2.4 48.9 %collective-permute-start = (bf16[32,30016]{1,0:T(8,128)(2,1)S(1)}, bf16[32,30016]{1,0:T(8,128)(2,1)S(1)}, u32[]{:S(2)}, u32[]{:S(2)}) collective-permute-start(bf16[32,30016]{1,0:T(8,128)(2,1)S(1)} %get-tuple-element.9), channel_id=1, source_target_pairs={{0,1},{1,2},{2,3},{3,4},{4,5},{5,6},{6,7},{7,0},{8,9},{9,10},{10,1... | collective-permute-start | bytes 5763080 | tf_op jit(solution)/shard_map/ppermute | solution.py:13
  5.4 87.1 %collective-permute-start.7 = (bf16[32,30016]{1,0:T(8,128)(2,1)S(1)}, bf16[32,30016]{1,0:T(8,128)(2,1)S(1)}, u32[]{:S(2)}, u32[]{:S(2)}) collective-permute-start(bf16[32,30016]{1,0:T(8,128)(2,1)S(1)} %get-tuple-element.8), channel_id=1, source_target_pairs={{0,1},{1,2},{2,3},{3,4},{4,5},{5,6},{6,7},{7,0},{8,9},{9,10},{10,1... | collective-permute-start | bytes 5763080 | tf_op jit(solution)/shard_map/ppermute | solution.py:13
  51.2 123.8 %copy-start.1 = (bf16[32,30016]{1,0:T(8,128)(2,1)}, bf16[32,30016]{1,0:T(8,128)(2,1)S(1)}, u32[]{:S(2)}) copy-start(bf16[32,30016]{1,0:T(8,128)(2,1)S(1)} %collective-permute-done) | copy-start | bytes 5763076
  51.2 82.5 %collective-permute-start.1 = (bf16[32,30016]{1,0:T(8,128)(2,1)S(1)}, bf16[32,30016]{1,0:T(8,128)(2,1)S(1)}, u32[]{:S(2)}, u32[]{:S(2)}) collective-permute-start(bf16[32,30016]{1,0:T(8,128)(2,1)S(1)} %collective-permute-done), channel_id=1, source_target_pairs={{0,1},{1,2},{2,3},{3,4},{4,5},{5,6},{6,7},{7,0},{8,9},{9,10},{10,1... | collective-permute-start | bytes 5763080 | tf_op jit(solution)/shard_map/ppermute | solution.py:13
  92.5 82.5 %collective-permute-start.8 = (bf16[32,30016]{1,0:T(8,128)(2,1)S(1)}, bf16[32,30016]{1,0:T(8,128)(2,1)S(1)}, u32[]{:S(2)}, u32[]{:S(2)}) collective-permute-start(bf16[32,30016]{1,0:T(8,128)(2,1)S(1)} %collective-permute-done.7), channel_id=1, source_target_pairs={{0,1},{1,2},{2,3},{3,4},{4,5},{5,6},{6,7},{7,0},{8,9},{9,10},{10,1... | collective-permute-start | bytes 5763080 | tf_op jit(solution)/shard_map/ppermute | solution.py:13
  133.7 123.8 %copy-start.5 = (bf16[32,30016]{1,0:T(8,128)(2,1)}, bf16[32,30016]{1,0:T(8,128)(2,1)S(1)}, u32[]{:S(2)}) copy-start(bf16[32,30016]{1,0:T(8,128)(2,1)S(1)} %collective-permute-done.1) | copy-start | bytes 5763076
  133.7 82.5 %collective-permute-start.2 = (bf16[32,30016]{1,0:T(8,128)(2,1)S(1)}, bf16[32,30016]{1,0:T(8,128)(2,1)S(1)}, u32[]{:S(2)}, u32[]{:S(2)}) collective-permute-start(bf16[32,30016]{1,0:T(8,128)(2,1)S(1)} %collective-permute-done.1), channel_id=1, source_target_pairs={{0,1},{1,2},{2,3},{3,4},{4,5},{5,6},{6,7},{7,0},{8,9},{9,10},{10,1... | collective-permute-start | bytes 5763080 | tf_op jit(solution)/shard_map/ppermute | solution.py:13
  175.0 1.3 copy-start.3
  175.0 82.5 %collective-permute-start.9 = (bf16[32,30016]{1,0:T(8,128)(2,1)S(1)}, bf16[32,30016]{1,0:T(8,128)(2,1)S(1)}, u32[]{:S(2)}, u32[]{:S(2)}) collective-permute-start(bf16[32,30016]{1,0:T(8,128)(2,1)S(1)} %collective-permute-done.8), channel_id=1, source_target_pairs={{0,1},{1,2},{2,3},{3,4},{4,5},{5,6},{6,7},{7,0},{8,9},{9,10},{10,1... | collective-permute-start | bytes 5763080 | tf_op jit(solution)/shard_map/ppermute | solution.py:13
  216.2 123.8 %copy-start.9 = (bf16[32,30016]{1,0:T(8,128)(2,1)}, bf16[32,30016]{1,0:T(8,128)(2,1)S(1)}, u32[]{:S(2)}) copy-start(bf16[32,30016]{1,0:T(8,128)(2,1)S(1)} %collective-permute-done.2) | copy-start | bytes 5763076
  216.2 82.5 %collective-permute-start.3 = (bf16[32,30016]{1,0:T(8,128)(2,1)S(1)}, bf16[32,30016]{1,0:T(8,128)(2,1)S(1)}, u32[]{:S(2)}, u32[]{:S(2)}) collective-permute-start(bf16[32,30016]{1,0:T(8,128)(2,1)S(1)} %collective-permute-done.2), channel_id=1, source_target_pairs={{0,1},{1,2},{2,3},{3,4},{4,5},{5,6},{6,7},{7,0},{8,9},{9,10},{10,1... | collective-permute-start | bytes 5763080 | tf_op jit(solution)/shard_map/ppermute | solution.py:13
  257.5 1.3 copy-start.7
  257.5 82.5 %collective-permute-start.10 = (bf16[32,30016]{1,0:T(8,128)(2,1)S(1)}, bf16[32,30016]{1,0:T(8,128)(2,1)S(1)}, u32[]{:S(2)}, u32[]{:S(2)}) collective-permute-start(bf16[32,30016]{1,0:T(8,128)(2,1)S(1)} %collective-permute-done.9), channel_id=1, source_target_pairs={{0,1},{1,2},{2,3},{3,4},{4,5},{5,6},{6,7},{7,0},{8,9},{9,10},{10,1... | collective-permute-start | bytes 5763080 | tf_op jit(solution)/shard_map/ppermute | solution.py:13
  298.7 123.9 %copy-start.13 = (bf16[32,30016]{1,0:T(8,128)(2,1)}, bf16[32,30016]{1,0:T(8,128)(2,1)S(1)}, u32[]{:S(2)}) copy-start(bf16[32,30016]{1,0:T(8,128)(2,1)S(1)} %collective-permute-done.3) | copy-start | bytes 5763076
  298.7 82.5 %collective-permute-start.4 = (bf16[32,30016]{1,0:T(8,128)(2,1)S(1)}, bf16[32,30016]{1,0:T(8,128)(2,1)S(1)}, u32[]{:S(2)}, u32[]{:S(2)}) collective-permute-start(bf16[32,30016]{1,0:T(8,128)(2,1)S(1)} %collective-permute-done.3), channel_id=1, source_target_pairs={{0,1},{1,2},{2,3},{3,4},{4,5},{5,6},{6,7},{7,0},{8,9},{9,10},{10,1... | collective-permute-start | bytes 5763080 | tf_op jit(solution)/shard_map/ppermute | solution.py:13
  340.0 1.3 copy-start.11
  340.0 82.6 %collective-permute-start.11 = (bf16[32,30016]{1,0:T(8,128)(2,1)S(1)}, bf16[32,30016]{1,0:T(8,128)(2,1)}, u32[]{:S(2)}, u32[]{:S(2)}) collective-permute-start(bf16[32,30016]{1,0:T(8,128)(2,1)S(1)} %collective-permute-done.10), channel_id=1, source_target_pairs={{0,1},{1,2},{2,3},{3,4},{4,5},{5,6},{6,7},{7,0},{8,9},{9,10},{10,1... | collective-permute-start | bytes 5763080 | tf_op jit(solution)/shard_map/ppermute | solution.py:13
  381.3 41.4 %copy-start.14 = (bf16[32,30016]{1,0:T(8,128)(2,1)}, bf16[32,30016]{1,0:T(8,128)(2,1)S(1)}, u32[]{:S(2)}) copy-start(bf16[32,30016]{1,0:T(8,128)(2,1)S(1)} %collective-permute-done.4) | copy-start | bytes 5763076
  381.3 82.6 %collective-permute-start.5 = (bf16[32,30016]{1,0:T(8,128)(2,1)S(1)}, bf16[32,30016]{1,0:T(8,128)(2,1)}, u32[]{:S(2)}, u32[]{:S(2)}) collective-permute-start(bf16[32,30016]{1,0:T(8,128)(2,1)S(1)} %collective-permute-done.4), channel_id=1, source_target_pairs={{0,1},{1,2},{2,3},{3,4},{4,5},{5,6},{6,7},{7,0},{8,9},{9,10},{10,1... | collective-permute-start | bytes 5763080 | tf_op jit(solution)/shard_map/ppermute | solution.py:13
  422.6 82.5 %collective-permute-start.12 = (bf16[32,30016]{1,0:T(8,128)(2,1)}, bf16[32,30016]{1,0:T(8,128)(2,1)}, u32[]{:S(2)}, u32[]{:S(2)}) collective-permute-start(bf16[32,30016]{1,0:T(8,128)(2,1)} %collective-permute-done.11), channel_id=1, source_target_pairs={{0,1},{1,2},{2,3},{3,4},{4,5},{5,6},{6,7},{7,0},{8,9},{9,10},{10,1... | collective-permute-start | bytes 5763080 | tf_op jit(solution)/shard_map/ppermute | solution.py:13
  463.9 82.5 %collective-permute-start.6 = (bf16[32,30016]{1,0:T(8,128)(2,1)}, bf16[32,30016]{1,0:T(8,128)(2,1)}, u32[]{:S(2)}, u32[]{:S(2)}) collective-permute-start(bf16[32,30016]{1,0:T(8,128)(2,1)} %collective-permute-done.5), channel_id=1, source_target_pairs={{0,1},{1,2},{2,3},{3,4},{4,5},{5,6},{6,7},{7,0},{8,9},{9,10},{10,1... | collective-permute-start | bytes 5763080 | tf_op jit(solution)/shard_map/ppermute | solution.py:13
  463.9 89.8 %copy-start.10 = (bf16[32,30016]{1,0:T(8,128)(2,1)S(1)}, bf16[32,30016]{1,0:T(8,128)(2,1)}, u32[]{:S(2)}) copy-start(bf16[32,30016]{1,0:T(8,128)(2,1)} %copy-done.9) | copy-start | bytes 5763076
  463.9 90.1 %copy-start.6 = (bf16[32,30016]{1,0:T(8,128)(2,1)S(1)}, bf16[32,30016]{1,0:T(8,128)(2,1)}, u32[]{:S(2)}) copy-start(bf16[32,30016]{1,0:T(8,128)(2,1)} %copy-done.5) | copy-start | bytes 5763076
  463.9 90.3 %copy-start.2 = (bf16[32,30016]{1,0:T(8,128)(2,1)S(1)}, bf16[32,30016]{1,0:T(8,128)(2,1)}, u32[]{:S(2)}) copy-start(bf16[32,30016]{1,0:T(8,128)(2,1)} %copy-done.1) | copy-start | bytes 5763076
  505.1 81.6 %collective-permute-start.13 = (bf16[32,30016]{1,0:T(8,128)(2,1)}, bf16[32,30016]{1,0:T(8,128)(2,1)S(1)}, u32[]{:S(2)}, u32[]{:S(2)}) collective-permute-start(bf16[32,30016]{1,0:T(8,128)(2,1)} %collective-permute-done.12), channel_id=1, source_target_pairs={{0,1},{1,2},{2,3},{3,4},{4,5},{5,6},{6,7},{7,0},{8,9},{9,10},{10,1... | collective-permute-start | bytes 5763080 | tf_op jit(solution)/shard_map/ppermute | solution.py:13
  549.8 44.1 %copy-start.12 = (bf16[32,30016]{1,0:T(8,128)(2,1)S(1)}, bf16[32,30016]{1,0:T(8,128)(2,1)}, u32[]{:S(2)}) copy-start(bf16[32,30016]{1,0:T(8,128)(2,1)} %copy-done.11) | copy-start | bytes 5763076
  551.7 43.6 %copy-start.8 = (bf16[32,30016]{1,0:T(8,128)(2,1)S(1)}, bf16[32,30016]{1,0:T(8,128)(2,1)}, u32[]{:S(2)}) copy-start(bf16[32,30016]{1,0:T(8,128)(2,1)} %copy-done.7) | copy-start | bytes 5763076
  553.7 43.1 %copy-start.4 = (bf16[32,30016]{1,0:T(8,128)(2,1)S(1)}, bf16[32,30016]{1,0:T(8,128)(2,1)}, u32[]{:S(2)}) copy-start(bf16[32,30016]{1,0:T(8,128)(2,1)} %copy-done.3) | copy-start | bytes 5763076
  554.2 45.4 %copy-start = (bf16[2,32,30016]{2,1,0:T(8,128)(2,1)S(1)}, bf16[2,32,30016]{2,1,0:T(8,128)(2,1)}, u32[]{:S(2)}) copy-start(bf16[2,32,30016]{2,1,0:T(8,128)(2,1)} %param.6) | copy-start | bytes 11526148
  601.2 5.4 copy-start.16
  606.6 20.8 %copy-start.15 = (f32[2,256,256]{2,1,0:T(8,128)S(1)}, f32[2,256,256]{2,1,0:T(8,128)}, u32[]{:S(2)}) copy-start(f32[2,256,256]{2,1,0:T(8,128)} %param.7) | copy-start | bytes 1572868
